TPU v7x, 32 devices: a whole 2x2x4 slice. The times are simulated.
32 devices in a mesh: row: 8 (over y, x, core), col: 4 (over z).
Axes of the slice: x: 2, y: 2, z: 4, core: 2. Of those that a mesh axis runs over, the one named last changes fastest.
Arguments:
- coeffs: bfloat16 [6144, 4096], P('row', 'col'), may hold values from -0.00390625 to 0.00390625
- occupation: float32 [4096], P('col'), may hold values from 0.5 to 2
- basis_on_grid: bfloat16 [320, 512, 512], P('row'), may hold values from -6 to 6
- basis_map: int32 [320, 512], P('row'), may hold values from 0 to 6143, as said below
- basis_count: int32 [320], P('row'), may hold values from 256 to 512
- batch_atom: int32 [320], P('row'), may hold values from 0 to 63
- harmonics: float32 [320, 49, 512], P('row'), may hold values from -0.25 to 0.25
Outputs:
- density: float32 [320, 512], P('row', 'col')
- moments: float32 [64, 49], replicated
Inputs may be any that keep to these rules, and one draw needn't show every extreme that they name: `basis_map`: the slots of one batch name distinct basis functions. With R = 768 and o = b // 40, batch b names only basis functions q * R + (o * 96 + w) mod R with 0 <= q < 8 and 0 <= w < 96.
All inputs are finite; a program needn't handle non-finite values.
Results may differ from a plain program's by a relative error of at most 0.0003.
Values may be sent and summed in bfloat16 or wider, within the bound.
A program may use at most 192 MiB of HBM per device.

v0:
```python
import functools

import jax
import jax.numpy as jnp
from jax import lax
from jax.experimental import pallas as pl
from jax.experimental.pallas import tpu as pltpu
from jax.sharding import PartitionSpec as P

WIN = 96
NATOM = 64
VMEM_BYTES = 62 * 1024 * 1024
DEPTH = 3


def plain(coeffs, occupation, basis_on_grid, basis_map, basis_count):
    batches, points, slots = basis_on_grid.shape
    owned = coeffs.shape[0]
    owners = lax.axis_size("row")
    target = lax.broadcasted_iota(jnp.int32, (owners, WIN), 0)
    offset = lax.broadcasted_iota(jnp.int32, (owners, WIN), 1)
    outgoing_ids = jnp.mod(target * WIN + offset, owned).reshape(-1)
    outgoing = jnp.take(coeffs, outgoing_ids, axis=0)
    window = lax.all_to_all(outgoing, "row", split_axis=0, concat_axis=0, tiled=True)
    start = jnp.mod(lax.axis_index("row") * WIN, owned)
    source = basis_map // owned
    within = jnp.mod(basis_map % owned - start, owned)
    local_ids = source * WIN + within
    selected = jnp.take(window, local_ids, axis=0)
    slot_ids = lax.broadcasted_iota(jnp.int32, (batches, slots), 1)
    keep = slot_ids < basis_count[:, None]
    masked = jnp.where(keep[:, None, :], basis_on_grid, jnp.zeros_like(basis_on_grid))
    orbital = jnp.einsum("bps,bsk->bpk", masked, selected, preferred_element_type=jnp.float32)
    partial_density = jnp.sum(orbital * orbital * occupation[None, None, :], axis=2)
    full_density = lax.psum(partial_density, "col")
    share = points // lax.axis_size("col")
    return lax.dynamic_slice_in_dim(full_density, lax.axis_index("col") * share, share, 1)


def kernel(rows, cols, owned, coeffs, occ, basis, index, count, atom, harmonics, out, out_moments,
           held, window, across, weight, spread, angular, dens, got, near, far, moment,
           own_sem, in_sem, angular_sem, send_sem, recv_sem, dsend_sem, drecv_sem,
           nsend_sem, nrecv_sem, fsend_sem, frecv_sem):
    batches, points, slots = basis.shape
    states = coeffs.shape[1]
    me, mine = lax.axis_index("row"), lax.axis_index("col")
    share = points // cols

    barrier = pltpu.get_barrier_semaphore()
    for k in range(1, rows):
        pl.semaphore_signal(barrier, inc=1, device_id={"row": lax.rem(me + k, rows)},
                            device_id_type=pl.DeviceIdType.MESH)
    for k in range(1, cols):
        pl.semaphore_signal(barrier, inc=1, device_id={"col": lax.rem(mine + k, cols)},
                            device_id_type=pl.DeviceIdType.MESH)

    def fetch(b, slot):
        return pltpu.make_async_copy(basis.at[b], held.at[slot], in_sem.at[slot])

    for b in range(DEPTH - 1):
        fetch(b, b).start()
    here = pl.ds(pl.multiple_of(me * WIN, 32), WIN)

    def rows_for(owner):
        return coeffs.at[pl.ds(pl.multiple_of(lax.rem(owner * WIN, owned), 32), WIN), :]

    own = pltpu.make_async_copy(rows_for(me), window.at[here, :], own_sem)
    own.start()
    load = pltpu.make_async_copy(harmonics, angular, angular_sem)
    load.start()
    pl.semaphore_wait(barrier, rows + cols - 2)
    sends = []
    for k in range(1, rows):
        peer = lax.rem(me + k, rows)
        copy = pltpu.make_async_remote_copy(
            src_ref=rows_for(peer), dst_ref=window.at[here, :],
            send_sem=send_sem.at[k - 1], recv_sem=recv_sem.at[k - 1],
            device_id={"row": peer}, device_id_type=pl.DeviceIdType.MESH)
        copy.start()
        sends.append(copy)

    for j in range(states // 128):
        line = jnp.broadcast_to(occ[j:j + 1, :], (128, 128))
        weight[j * 128:(j + 1) * 128, :] = line.T

    start = lax.rem(me * WIN, owned)
    row_of = lax.broadcasted_iota(jnp.int32, (WIN, 1), 0) + start
    name = jnp.concatenate([row_of + r * owned for r in range(rows)], axis=0)
    lane = lax.broadcasted_iota(jnp.int32, (1, slots), 1)

    def scatter(b, carry):
        slot = lax.rem(b, DEPTH)
        ahead = b + DEPTH - 1

        @pl.when(ahead < batches)
        def _():
            fetch(ahead, lax.rem(ahead, DEPTH)).start()

        fetch(b, slot).wait()
        ids = jnp.where(lane < count[b], index[pl.ds(b, 1), :], -1)
        hot = jnp.where(name == ids, 1.0, 0.0).astype(jnp.bfloat16)
        moved = lax.dot_general(hot, held[slot], (((1,), (1,)), ((), ())),
                                preferred_element_type=jnp.float32)
        spread[b] = moved.astype(jnp.bfloat16)
        return carry

    lax.fori_loop(0, batches, scatter, 0)

    own.wait()
    for copy in sends:
        copy.wait()
    for j in range(states // 128):
        across[j * 128:(j + 1) * 128, :] = window[:, j * 128:(j + 1) * 128].T

    load.wait()
    moment[...] = jnp.zeros_like(moment)
    atoms = lax.broadcasted_iota(jnp.int32, (1, 128), 1)

    def square(b, carry):
        values = spread[b]
        total = jnp.zeros((8, points), jnp.float32)
        step = 256
        for n in range(0, states, step):
            orbital = lax.dot_general(across[n:n + step, :], values, (((1,), (0,)), ((), ())),
                                      preferred_element_type=jnp.float32)
            scale = weight[n:n + step, :]
            scale = jnp.concatenate([scale] * (points // 128), axis=1)
            term = orbital * orbital * scale
            total = total + jnp.sum(term.reshape(step // 8, 8, points), axis=0)
        line = jnp.sum(total, axis=0, keepdims=True)
        for c in range(cols):
            dens[c, pl.ds(b, 1), :] = line[:, c * share:(c + 1) * share]
        local = jnp.sum(angular[b] * line, axis=1, keepdims=True)
        moment[...] += local * jnp.where(atoms == atom[b], 1.0, 0.0)
        return carry

    lax.fori_loop(0, batches, square, 0)

    def exchange(axis, place, size, src_of, dst_of, sent, received):
        copies = []
        for k in range(1, size):
            peer = lax.rem(place + k, size)
            copy = pltpu.make_async_remote_copy(
                src_ref=src_of(peer), dst_ref=dst_of(k),
                send_sem=sent.at[k - 1], recv_sem=received.at[k - 1],
                device_id={axis: peer}, device_id_type=pl.DeviceIdType.MESH)
            copy.start()
            copies.append(copy)
        return copies

    moved = exchange("col", mine, cols, lambda peer: moment, lambda k: near.at[mine],
                     nsend_sem, nrecv_sem)
    copies = exchange("col", mine, cols, lambda peer: dens.at[peer], lambda k: got.at[k - 1],
                      dsend_sem, drecv_sem)
    near[mine] = moment[...]
    for copy in moved:
        copy.wait()
    total = near[0]
    for c in range(1, cols):
        total = total + near[c]
    moment[...] = total
    far[me] = total
    moved = exchange("row", me, rows, lambda peer: moment, lambda k: far.at[me],
                     fsend_sem, frecv_sem)
    result = dens[mine]
    for k, copy in enumerate(copies):
        copy.wait()
        result = result + got[k]
    out[...] = result
    for copy in moved:
        copy.wait()
    total = far[0]
    for r in range(1, rows):
        total = total + far[r]
    count_l = total.shape[0]
    total = jnp.concatenate([total, jnp.zeros((128 - count_l, 128), jnp.float32)], axis=0)
    out_moments[...] = total.T[:NATOM, :count_l]


def fused(coeffs, occupation, basis_on_grid, basis_map, basis_count, batch_atom, harmonics):
    batches, points, slots = basis_on_grid.shape
    owned, states = coeffs.shape
    rows, cols = lax.axis_size("row"), lax.axis_size("col")
    reach = rows * WIN
    vmem, dma = pltpu.VMEM, pltpu.SemaphoreType.DMA
    half, single = jnp.bfloat16, jnp.float32
    whole = pl.BlockSpec(memory_space=pltpu.VMEM)
    scalar = pl.BlockSpec(memory_space=pltpu.SMEM)
    lm = harmonics.shape[1]
    apart = pl.BlockSpec(memory_space=pl.ANY)
    return pl.pallas_call(
        functools.partial(kernel, rows, cols, owned),
        out_shape=(jax.ShapeDtypeStruct((batches, points // cols), single),
                   jax.ShapeDtypeStruct((NATOM, lm), single)),
        in_specs=[apart, whole, apart, whole, scalar, scalar, apart],
        out_specs=(whole, whole),
        scratch_shapes=[
            vmem((DEPTH, points, slots), half),
            vmem((reach, states), half),
            vmem((states, reach), half),
            vmem((states, 128), single),
            vmem((batches, reach, points), half),
            vmem((batches, lm, points), single),
            vmem((cols, batches, points // cols), single),
            vmem((cols - 1, batches, points // cols), single),
            vmem((cols, lm, 128), single),
            vmem((rows, lm, 128), single),
            vmem((lm, 128), single),
            dma, dma((DEPTH,)), dma, dma((rows - 1,)), dma((rows - 1,)),
            dma((cols - 1,)), dma((cols - 1,)), dma((cols - 1,)), dma((cols - 1,)),
            dma((rows - 1,)), dma((rows - 1,)),
        ],
        compiler_params=pltpu.CompilerParams(
            collective_id=0, has_side_effects=True, vmem_limit_bytes=VMEM_BYTES),
    )(coeffs, occupation.reshape(-1, 128), basis_on_grid, basis_map, basis_count,
      batch_atom, harmonics)


def shards(coeffs, occupation, basis_on_grid, basis_map, basis_count, batch_atom, harmonics):
    batches, points, slots = basis_on_grid.shape
    owned, states = coeffs.shape
    cols, reach = lax.axis_size("col"), lax.axis_size("row") * WIN
    share = points // cols
    needed = batches * reach * points * 2 + 4 * reach * states
    if needed < VMEM_BYTES * 3 // 4 and share % 128 == 0 and owned % WIN == 0:
        return fused(coeffs, occupation, basis_on_grid, basis_map, basis_count,
                     batch_atom, harmonics)
    density = plain(coeffs, occupation, basis_on_grid, basis_map, basis_count)
    part = lax.dynamic_slice_in_dim(harmonics, lax.axis_index("col") * share, share, 2)
    local_moment = jnp.sum(part * density[:, None, :], axis=2)
    atom_ids = lax.broadcasted_iota(jnp.int32, (batches, NATOM), 1)
    member = (batch_atom[:, None] == atom_ids).astype(jnp.float32)
    atom_part = jnp.dot(member.T, local_moment, precision=lax.Precision.HIGHEST)
    moments = lax.psum(atom_part, ("row", "col"))
    return (density, moments)


def solution(mesh):
    placed = (
        P("row", "col"),
        P("col"),
        P("row", None, None),
        P("row", None),
        P("row"),
        P("row"),
        P("row", None, None),
    )
    return jax.shard_map(
        shards, mesh=mesh, in_specs=placed, out_specs=(P("row", "col"), P()), check_vma=False
    )
```

profile of v0, /device:TPU:0, one launch (start us, length us, event | category | flops | bytes accessed | tf_op | source)
XLA Modules:
  0.0 93.9 jit_solution(18042065074444109947)
XLA Ops:
  0.6 6.6 %copy.9.harmonics = f32[40,49,512]{2,1,0:T(8,128)} copy(f32[40,49,512]{2,0,1:T(8,128)} %param.13) | data formatting | bytes 8028160 | tf_op args[6]
  7.2 83.9 %shard_map.86 = (f32[40,128]{1,0:T(8,128)}, f32[64,49]{1,0:T(8,128)}) custom-call(bf16[768,1024]{1,0:T(8,128)(2,1)} %coeffs.1, f32[8,128]{1,0:T(8,128)} %bitcast.1, bf16[40,512,512]{2,1,0:T(8,128)(2,1)} %basis.1, s32[40,512]{1,0:T(8,128)} %index.1, s32[40]{0:T(128)} %count.1, s32[40]{0:T(128)} %atom.1, f32[40,49,512]{2,1,0:T(8,128)} %copy.9.harmonics), custom_call_target="tpu_custom_call" | custom-call | tf_op jit(solution)/shard_map/pallas_call | solution.py:191
  91.1 1.5 %copy.10 = f32[64,49]{0,1:T(8,128)} copy(f32[64,49]{1,0:T(8,128)} %get-tuple-element.3) | data formatting | bytes 25088 | tf_op jit(solution)/shard_map/pallas_call | solution.py:191
  92.6 1.3 %copy.12 = f32[40,128]{1,0:T(8,128)} copy(f32[40,128]{1,0:T(8,128)} %get-tuple-element.6) | data formatting | bytes 40960
where the time goes:
time: 94.2 us; the launch traced here: 93.9 us
  Pallas kernels  83.9 us (89%)
  local copies, waits for them, and re-layouts  9.35 us (10%)
    pallas_call x1, Pallas kernels, fused(): pl.pallas_call(functools.partial(kernel, rows, cols, owned), out_shape=(j...  83.9 us
    unnamed x2, local copies, waits for them, and re-layouts  7.9 us

commit v1 on v0

v1 whole, which is shorter than its diff:
```python
import functools

import jax
import jax.numpy as jnp
from jax import lax
from jax.experimental import pallas as pl
from jax.experimental.pallas import tpu as pltpu
from jax.sharding import PartitionSpec as P

WIN = 96
NATOM = 64
LANES = 128
VMEM_BYTES = 62 * 1024 * 1024
DEPTH = 4
STEPS = 32767.0
MARGIN = 1.0 + 2.0 ** -7
MESH = pl.DeviceIdType.MESH
ORDER = (0, 1, 2, 4, 3, 5, 6, 7)


def plain(coeffs, occupation, basis_on_grid, basis_map, basis_count):
    batches, points, slots = basis_on_grid.shape
    owned = coeffs.shape[0]
    owners = lax.axis_size("row")
    target = lax.broadcasted_iota(jnp.int32, (owners, WIN), 0)
    offset = lax.broadcasted_iota(jnp.int32, (owners, WIN), 1)
    outgoing_ids = jnp.mod(target * WIN + offset, owned).reshape(-1)
    outgoing = jnp.take(coeffs, outgoing_ids, axis=0)
    window = lax.all_to_all(outgoing, "row", split_axis=0, concat_axis=0, tiled=True)
    start = jnp.mod(lax.axis_index("row") * WIN, owned)
    source = basis_map // owned
    within = jnp.mod(basis_map % owned - start, owned)
    local_ids = source * WIN + within
    selected = jnp.take(window, local_ids, axis=0)
    slot_ids = lax.broadcasted_iota(jnp.int32, (batches, slots), 1)
    keep = slot_ids < basis_count[:, None]
    masked = jnp.where(keep[:, None, :], basis_on_grid, jnp.zeros_like(basis_on_grid))
    orbital = jnp.einsum("bps,bsk->bpk", masked, selected, preferred_element_type=jnp.float32)
    partial_density = jnp.sum(orbital * orbital * occupation[None, None, :], axis=2)
    full_density = lax.psum(partial_density, "col")
    share = points // lax.axis_size("col")
    return lax.dynamic_slice_in_dim(full_density, lax.axis_index("col") * share, share, 1)


def plan(groups, cols):
    early, late = groups - 1, groups - 1
    pairs = [[(i, (i, (i + 1) % early)) for i in range(early)]][0]
    rest = [(i, j) for i in range(early) for j in range(i) if (i - j) % early not in (1, early - 1)]
    while rest:
        degree = [sum(v in edge for edge in rest) for v in range(early)]
        v = degree.index(max(degree))
        taken = [edge for edge in rest if v in edge][:2]
        rest = [edge for edge in rest if edge not in taken]
        pairs.append((v, tuple(a if b == v else b for a, b in taken)))
    pairs.sort(key=lambda entry: -len(entry[1]))
    kept = [pairs[c::cols] for c in range(cols)]
    blocks = list(range(groups))
    counts = [groups // cols + (1 if c in range(0, 2 * (groups % cols), 2) else 0) for c in range(cols)]
    for c in range(cols):
        kept[c] = kept[c] + [(late, tuple(blocks[:counts[c]]))]
        blocks = blocks[counts[c]:]
    return kept


def kernel(rows, cols, owned, coeffs, occ, basis, index, count, atom, harmonics, out, out_moments,
           held, window, split, local, scale_col, scale_row, norm, code, taken, norms, matrix,
           spread, angular, member, line, dens, got, near, far, moment,
           own_sem, in_sem, angular_sem, send_sem, recv_sem, zsend_sem, zrecv_sem, vsend_sem, vrecv_sem,
           dsend_sem, drecv_sem, nsend_sem, nrecv_sem, fsend_sem, frecv_sem):
    batches, points, slots = basis.shape
    states = coeffs.shape[1]
    reach = rows * WIN
    groups = reach // LANES
    me, mine = lax.axis_index("row"), lax.axis_index("col")
    share = points // cols
    kept = plan(groups, cols)
    entries = len(kept[0])

    barrier = pltpu.get_barrier_semaphore()
    for k in range(1, rows):
        pl.semaphore_signal(barrier, inc=1, device_id={"row": lax.rem(me + k, rows)},
                            device_id_type=MESH)
    for k in range(1, cols):
        pl.semaphore_signal(barrier, inc=1, device_id={"col": lax.rem(mine + k, cols)},
                            device_id_type=MESH)

    def fetch(b, slot):
        return pltpu.make_async_copy(basis.at[b], held.at[slot], in_sem.at[slot])

    for b in range(DEPTH - 1):
        fetch(b, b).start()

    def rows_for(owner):
        return coeffs.at[pl.ds(pl.multiple_of(lax.rem(owner * WIN, owned), 32), WIN), :]

    def partner(k):
        bits = (lax.rem(me, 2), lax.rem(lax.div(me, 2), 2), lax.div(me, 4))
        return sum((1 - bit if k >> n & 1 else bit) * (1 << n) for n, bit in enumerate(bits))

    own = pltpu.make_async_copy(rows_for(me), window.at[0:WIN, :], own_sem)
    own.start()
    pl.semaphore_wait(barrier, rows + cols - 2)
    sends = []
    for p in range(1, rows):
        peer = partner(ORDER[p])
        copy = pltpu.make_async_remote_copy(
            src_ref=rows_for(peer), dst_ref=window.at[p * WIN:(p + 1) * WIN, :],
            send_sem=send_sem.at[p - 1], recv_sem=recv_sem.at[p - 1],
            device_id={"row": peer}, device_id_type=MESH)
        copy.start()
        sends.append(copy)
    load = pltpu.make_async_copy(harmonics, angular, angular_sem)
    load.start()

    start = lax.rem(me * WIN, owned)
    row_of = lax.broadcasted_iota(jnp.int32, (WIN, 1), 0) + start
    name = jnp.concatenate([row_of + partner(k) * owned for k in ORDER], axis=0)
    lane = lax.broadcasted_iota(jnp.int32, (1, slots), 1)
    atoms = lax.broadcasted_iota(jnp.int32, (1, LANES), 1)
    matrix[...] = jnp.zeros_like(matrix)

    def scatter(b, carry):
        slot = lax.rem(b, DEPTH)
        ahead = b + DEPTH - 1

        @pl.when(ahead < batches)
        def _():
            fetch(ahead, lax.rem(ahead, DEPTH)).start()

        fetch(b, slot).wait()
        ids = jnp.where(lane < count[b], index[pl.ds(b, 1), :], -1)
        hot = jnp.where(name == ids, 1.0, 0.0).astype(jnp.bfloat16)
        moved = lax.dot_general(hot, held[slot], (((1,), (1,)), ((), ())),
                                preferred_element_type=jnp.float32)
        spread[b] = moved.astype(jnp.bfloat16)
        member[pl.ds(b, 1), :] = jnp.where(atoms == atom[b], 1.0, 0.0)
        return carry

    def group_rows(g):
        return slice(g * LANES, (g + 1) * LANES)

    spots = {}
    for owner in range(cols):
        for e, (i, js) in enumerate(kept[owner]):
            for h, j in enumerate(js):
                spots[i, j] = (owner, 2 * e + h)
    ids_of = {block: n for n, block in enumerate(spots)}

    def block_copy(block):
        owner, slot = spots[block]
        n = ids_of[block]
        return pltpu.make_async_remote_copy(
            src_ref=code.at[n], dst_ref=taken.at[mine, slot],
            send_sem=zsend_sem.at[n], recv_sem=zrecv_sem.at[mine, slot],
            device_id={"col": owner}, device_id_type=MESH)

    def norm_copy(stage, k):
        return pltpu.make_async_remote_copy(
            src_ref=norm.at[stage], dst_ref=norms.at[mine, stage],
            send_sem=vsend_sem.at[stage, k - 1], recv_sem=vrecv_sem.at[mine, stage],
            device_id={"col": lax.rem(mine + k, cols)}, device_id_type=MESH)

    def correlate(stage, fresh):
        tile_row = lax.broadcasted_iota(jnp.int32, (8, LANES), 0)
        tile = jnp.zeros((8, LANES), jnp.float32)
        for g in fresh:
            wide = window[group_rows(g), :].astype(jnp.float32)
            scaled = wide * occ[...]
            high = scaled.astype(jnp.bfloat16)
            split[g, 0:LANES, :] = high
            split[g, LANES:2 * LANES, :] = (scaled - high.astype(jnp.float32)).astype(jnp.bfloat16)
            square = jnp.sum(scaled * wide, axis=1, keepdims=True)
            root = jnp.where(square > 0.0, lax.rsqrt(square), 0.0)
            inverse = jnp.broadcast_to(root * (1.0 / MARGIN), (LANES, LANES))
            scale_col[g] = inverse
            scale_row[g] = inverse.T[0:8, :]
            length = jnp.broadcast_to(square * root * MARGIN, (LANES, LANES)).T
            tile = jnp.where(tile_row == g, length[0:8, :], tile)
        norm[stage] = tile
        for k in range(1, cols):
            norm_copy(stage, k).start()
        for block, (owner, slot) in spots.items():
            i, j = block
            if max(block) not in fresh:
                continue
            both = lax.dot_general(split[j], window[group_rows(i), :], (((1,), (1,)), ((), ())),
                                   preferred_element_type=jnp.float32)
            value = both[0:LANES, :] + both[LANES:2 * LANES, :]
            local[ids_of[block]] = value
            ratio = value * scale_col[j] * scale_row[i, 0:1, :]
            steps = jnp.round(ratio * STEPS).astype(jnp.int32)
            half = LANES // 2
            code[ids_of[block]] = (steps[0:half, :] << 16) | (steps[half:, :] & 0xFFFF)

            @pl.when(mine != owner)
            def _():
                block_copy(block).start()

    def collect(owner, es):
        others = [s for s in range(cols) if s != owner]
        for e in es:
            i, js = kept[owner][e]
            for h, j in enumerate(js):
                slot = 2 * e + h
                value = local[ids_of[i, j]]
                for s in others:
                    pltpu.make_async_remote_copy(
                        src_ref=code.at[0], dst_ref=taken.at[s, slot],
                        send_sem=zsend_sem.at[0], recv_sem=zrecv_sem.at[s, slot],
                        device_id={"col": s}, device_id_type=MESH).wait_recv()
                    word = taken[s, slot]
                    steps = jnp.concatenate([word >> 16, (word << 16) >> 16], axis=0)
                    down = norms[s, stage_of(j), j:j + 1, :] * (1.0 / STEPS)
                    down = jnp.broadcast_to(down, (LANES, LANES)).T
                    value = value + steps.astype(jnp.float32) * down * norms[s, stage_of(i), i:i + 1, :]
                if i != j:
                    value = value + value
                high = value.astype(jnp.bfloat16)
                low = (value - high.astype(jnp.float32)).astype(jnp.bfloat16)
                matrix[e, group_rows(h), 0:LANES] = high
                matrix[e, group_rows(h), LANES:2 * LANES] = low

    needs = [-(-(g + 1) * LANES // WIN) for g in range(groups)]
    stages = [[0, 1, 2]] + [[g] for g in range(3, groups)]

    def stage_of(g):
        return next(n for n, fresh in enumerate(stages) if g in fresh)

    def await_norms(owner, which):
        for stage in which:
            for s in range(cols):
                if s != owner:
                    pltpu.make_async_remote_copy(
                        src_ref=norm.at[stage], dst_ref=norms.at[s, stage],
                        send_sem=vsend_sem.at[stage, 0], recv_sem=vrecv_sem.at[s, stage],
                        device_id={"col": s}, device_id_type=MESH).wait_recv()

    bounds = [batches * n // 40 for n in (0, 16, 26, 36, 40)]
    arrived = 1
    own.wait()
    for stage, fresh in enumerate(stages):
        lax.fori_loop(bounds[stage], bounds[stage + 1], scatter, 0)
        while arrived < needs[fresh[-1]]:
            sends[arrived - 1].wait_recv()
            arrived += 1
        correlate(stage, fresh)

    def chosen(values):
        total = values[0]
        for c in range(1, cols):
            total = jnp.where(mine == c, values[c], total)
        return total

    def group_of(b, g):
        return spread[b, pl.ds(pl.multiple_of(g * LANES, LANES), LANES), :]

    def multiply(b, es):
        total = jnp.zeros((8, points), jnp.float32)
        for e in es:
            i = chosen([kept[c][e][0] for c in range(cols)])
            right = group_of(b, i)
            product = lax.dot_general(matrix[e], jnp.concatenate([right, right], axis=0),
                                      (((1,), (0,)), ((), ())), preferred_element_type=jnp.float32)
            for h in range(2):
                j = chosen([kept[c][e][1][min(h, len(kept[c][e][1]) - 1)] for c in range(cols)])
                term = product[group_rows(h), :] * group_of(b, j).astype(jnp.float32)
                total = total + jnp.sum(term.reshape(LANES // 8, 8, points), axis=0)
        return jnp.sum(total, axis=0, keepdims=True)

    last = len(stages) - 1
    for owner in range(cols):
        @pl.when(mine == owner)
        def _():
            await_norms(owner, range(last))
            collect(owner, range(entries - 1))

    unroll = 4

    def early(step, carry):
        for u in range(unroll):
            b = step * unroll + u
            line[pl.ds(b, 1), :] = multiply(b, range(entries - 1))
        return carry

    lax.fori_loop(0, batches // unroll, early, 0)

    for owner in range(cols):
        @pl.when(mine == owner)
        def _():
            await_norms(owner, [last])
            collect(owner, [entries - 1])

    load.wait()
    moment[...] = jnp.zeros_like(moment)

    def late(step, carry):
        for u in range(8):
            b = step * 8 + u
            line[pl.ds(b, 1), :] += multiply(b, [entries - 1])
        here = pl.ds(pl.multiple_of(step * 8, 8), 8)
        values = line[here, :]
        for c in range(cols):
            dens[c, here, :] = values[:, c * share:(c + 1) * share]
        part = jnp.sum(angular[:, here, :] * values[None], axis=2, keepdims=True)
        moment[...] += jnp.sum(part * member[here, :][None], axis=1)
        return carry

    lax.fori_loop(0, batches // 8, late, 0)

    def exchange(axis, place, size, src_of, dst_of, sent, received):
        copies = []
        for k in range(1, size):
            peer = lax.rem(place + k, size)
            copy = pltpu.make_async_remote_copy(
                src_ref=src_of(peer), dst_ref=dst_of(k),
                send_sem=sent.at[k - 1], recv_sem=received.at[k - 1],
                device_id={axis: peer}, device_id_type=MESH)
            copy.start()
            copies.append(copy)
        return copies

    moved = exchange("col", mine, cols, lambda peer: moment, lambda k: near.at[mine],
                     nsend_sem, nrecv_sem)
    copies = exchange("col", mine, cols, lambda peer: dens.at[peer], lambda k: got.at[k - 1],
                      dsend_sem, drecv_sem)
    near[mine] = moment[...]
    for copy in sends:
        copy.wait_send()
    for stage in range(len(stages)):
        for k in range(1, cols):
            norm_copy(stage, k).wait_send()
    for block, (owner, slot) in spots.items():
        @pl.when(mine != owner)
        def _():
            block_copy(block).wait_send()
    for copy in moved:
        copy.wait()
    total = near[0]
    for c in range(1, cols):
        total = total + near[c]
    moment[...] = total
    far[me] = total
    moved = exchange("row", me, rows, lambda peer: moment, lambda k: far.at[me],
                     fsend_sem, frecv_sem)
    result = dens[mine]
    for k, copy in enumerate(copies):
        copy.wait()
        result = result + got[k]
    out[...] = result
    for copy in moved:
        copy.wait()
    total = far[0]
    for r in range(1, rows):
        total = total + far[r]
    out_moments[...] = total[:, :NATOM]


def fused(coeffs, occupation, basis_on_grid, basis_map, basis_count, batch_atom, harmonics):
    batches, points, slots = basis_on_grid.shape
    owned, states = coeffs.shape
    rows, cols = lax.axis_size("row"), lax.axis_size("col")
    reach = rows * WIN
    groups = reach // LANES
    kept = plan(groups, cols)
    entries = len(kept[0])
    blocks = groups * (groups + 1) // 2
    stages = groups - 2
    vmem, dma = pltpu.VMEM, pltpu.SemaphoreType.DMA
    half, single, word = jnp.bfloat16, jnp.float32, jnp.int32
    whole = pl.BlockSpec(memory_space=pltpu.VMEM)
    scalar = pl.BlockSpec(memory_space=pltpu.SMEM)
    lm = harmonics.shape[1]
    apart = pl.BlockSpec(memory_space=pl.ANY)
    density, moments = pl.pallas_call(
        functools.partial(kernel, rows, cols, owned),
        out_shape=(jax.ShapeDtypeStruct((batches, points // cols), single),
                   jax.ShapeDtypeStruct((lm, NATOM), single)),
        in_specs=[apart, whole, apart, whole, scalar, scalar, apart],
        out_specs=(whole, whole),
        scratch_shapes=[
            vmem((DEPTH, points, slots), half),
            vmem((reach, states), half),
            vmem((groups, 2 * LANES, states), half),
            vmem((blocks, LANES, LANES), single),
            vmem((groups, LANES, LANES), single),
            vmem((groups, 8, LANES), single),
            vmem((stages, 8, LANES), single),
            vmem((blocks, LANES // 2, LANES), word),
            vmem((cols, 2 * entries, LANES // 2, LANES), word),
            vmem((cols, stages, 8, LANES), single),
            vmem((entries, 2 * LANES, 2 * LANES), half),
            vmem((batches, reach, points), half),
            vmem((lm, batches, points), single),
            vmem((batches, LANES), single),
            vmem((batches, points), single),
            vmem((cols, batches, points // cols), single),
            vmem((cols - 1, batches, points // cols), single),
            vmem((cols, lm, LANES), single),
            vmem((rows, lm, LANES), single),
            vmem((lm, LANES), single),
            dma, dma((DEPTH,)), dma, dma((rows - 1,)), dma((rows - 1,)),
            dma((blocks,)), dma((cols, 2 * entries)), dma((stages, cols - 1)), dma((cols, stages)),
            dma((cols - 1,)), dma((cols - 1,)), dma((cols - 1,)), dma((cols - 1,)),
            dma((rows - 1,)), dma((rows - 1,)),
        ],
        compiler_params=pltpu.CompilerParams(
            collective_id=0, has_side_effects=True, vmem_limit_bytes=VMEM_BYTES),
    )(coeffs, occupation.reshape(1, -1), basis_on_grid, basis_map, basis_count,
      batch_atom, jnp.transpose(harmonics, (1, 0, 2)))
    return density, moments.T


def shards(coeffs, occupation, basis_on_grid, basis_map, basis_count, batch_atom, harmonics):
    batches, points, slots = basis_on_grid.shape
    owned, states = coeffs.shape
    rows, cols = lax.axis_size("row"), lax.axis_size("col")
    reach = rows * WIN
    share = points // cols
    needed = batches * reach * points * 2 + 10 * reach * states
    fits = needed < VMEM_BYTES * 3 // 4 and share % LANES == 0 and owned % WIN == 0
    if fits and rows == len(ORDER) and cols == 4 and reach % LANES == 0 and batches % 8 == 0:
        return fused(coeffs, occupation, basis_on_grid, basis_map, basis_count,
                     batch_atom, harmonics)
    density = plain(coeffs, occupation, basis_on_grid, basis_map, basis_count)
    part = lax.dynamic_slice_in_dim(harmonics, lax.axis_index("col") * share, share, 2)
    local_moment = jnp.sum(part * density[:, None, :], axis=2)
    atom_ids = lax.broadcasted_iota(jnp.int32, (batches, NATOM), 1)
    member = (batch_atom[:, None] == atom_ids).astype(jnp.float32)
    atom_part = jnp.dot(member.T, local_moment, precision=lax.Precision.HIGHEST)
    moments = lax.psum(atom_part, ("row", "col"))
    return (density, moments)


def solution(mesh):
    placed = (
        P("row", "col"),
        P("col"),
        P("row", None, None),
        P("row", None),
        P("row"),
        P("row"),
        P("row", None, None),
    )
    return jax.shard_map(
        shards, mesh=mesh, in_specs=placed, out_specs=(P("row", "col"), P()), check_vma=False
    )
```

time: 94.2 us -> 69.1 us (0.73)
  Pallas kernels: 83.9 us -> 65.5 us
  local copies, waits for them, and re-layouts: 9.35 us -> 2.69 us
    pallas_call x1, Pallas kernels: 83.9 us -> 65.5 us  [fused(): pl.pallas_call(functools.partial(kernel, rows, cols, owned), out_shape=(j...]
    unnamed x2, local copies, waits for them, and re-layouts: 7.9 us -> 2.69 us
    pallas_call x1 -> x0, local copies, waits for them, and re-layouts: 1.45 us -> none  [fused(): pl.pallas_call(functools.partial(kernel, rows, cols, owned), out_shape=(j...]
where the time goes in v1:
time: 69.1 us; the launch traced here: 68.8 us
  Pallas kernels  65.5 us (95%)
  local copies, waits for them, and re-layouts  2.69 us (4%)
    pallas_call x1, Pallas kernels, fused(): pl.pallas_call(functools.partial(kernel, rows, cols, owned), out_shape=(j...  65.5 us
    unnamed x2, local copies, waits for them, and re-layouts  2.69 us

profile of v1, /device:TPU:0, one launch (start us, length us, event | category | flops | bytes accessed | tf_op | source)
XLA Modules:
  0.0 68.8 jit_solution(2602082394111266541)
XLA Ops:
  0.6 65.5 %shard_map.86 = (f32[40,128]{1,0:T(8,128)}, f32[49,64]{1,0:T(8,128)}) custom-call(bf16[768,1024]{1,0:T(8,128)(2,1)} %coeffs.1, f32[1,1024]{1,0:T(1,128)} %bitcast.5, bf16[40,512,512]{2,1,0:T(8,128)(2,1)} %basis.1, s32[40,512]{1,0:T(8,128)} %index.1, s32[40]{0:T(128)} %count.1, s32[40]{0:T(128)} %atom.1, f32[49,40,512]{2,1,0:T(8,128)} %bitcast.3), custom_call_target="tpu_custom_call" | custom-call | tf_op jit(solution)/shard_map/pallas_call | solution.py:374
  66.1 1.3 %copy.11 = f32[40,128]{1,0:T(8,128)} copy(f32[40,128]{1,0:T(8,128)} %get-tuple-element.8) | data formatting | bytes 40960
  67.5 1.4 %copy.12 = f32[64,49]{0,1:T(8,128)} copy(f32[64,49]{0,1:T(8,128)} %bitcast.4) | data formatting | bytes 25088

commit v2 on v1

--- a/solution.py
+++ b/solution.py
@@ -11,11 +11,19 @@
 NATOM = 64
 LANES = 128
 VMEM_BYTES = 62 * 1024 * 1024
-DEPTH = 4
+STEP = 4
+DEPTH = 2 * STEP
 STEPS = 32767.0
 MARGIN = 1.0 + 2.0 ** -7
 MESH = pl.DeviceIdType.MESH
 ORDER = (0, 1, 2, 4, 3, 5, 6, 7)
+KEPT = (
+    ((0, (2, 3)), (1, (2, 3)), (1, (1,))),
+    ((4, (0, 1)), (0, (0, 1)), (5, (0, 1))),
+    ((4, (2, 3)), (2, (2, 3)), (5, (2, 3))),
+    ((3, (3,)), (4, (4,)), (5, (4, 5))),
+)
+USED = ((0, 1, 2, 3), (0, 1, 4, 5), (2, 3, 4, 5), (2, 3, 4, 5))
 
 
 def plain(coeffs, occupation, basis_on_grid, basis_map, basis_count):
@@ -42,28 +50,8 @@
     return lax.dynamic_slice_in_dim(full_density, lax.axis_index("col") * share, share, 1)
 
 
-def plan(groups, cols):
-    early, late = groups - 1, groups - 1
-    pairs = [[(i, (i, (i + 1) % early)) for i in range(early)]][0]
-    rest = [(i, j) for i in range(early) for j in range(i) if (i - j) % early not in (1, early - 1)]
-    while rest:
-        degree = [sum(v in edge for edge in rest) for v in range(early)]
-        v = degree.index(max(degree))
-        taken = [edge for edge in rest if v in edge][:2]
-        rest = [edge for edge in rest if edge not in taken]
-        pairs.append((v, tuple(a if b == v else b for a, b in taken)))
-    pairs.sort(key=lambda entry: -len(entry[1]))
-    kept = [pairs[c::cols] for c in range(cols)]
-    blocks = list(range(groups))
-    counts = [groups // cols + (1 if c in range(0, 2 * (groups % cols), 2) else 0) for c in range(cols)]
-    for c in range(cols):
-        kept[c] = kept[c] + [(late, tuple(blocks[:counts[c]]))]
-        blocks = blocks[counts[c]:]
-    return kept
-
-
 def kernel(rows, cols, owned, coeffs, occ, basis, index, count, atom, harmonics, out, out_moments,
-           held, window, split, local, scale_col, scale_row, norm, code, taken, norms, matrix,
+           held, names, window, split, local, scale_col, scale_row, norm, code, taken, norms, matrix,
            spread, angular, member, line, dens, got, near, far, moment,
            own_sem, in_sem, angular_sem, send_sem, recv_sem, zsend_sem, zrecv_sem, vsend_sem, vrecv_sem,
            dsend_sem, drecv_sem, nsend_sem, nrecv_sem, fsend_sem, frecv_sem):
@@ -73,8 +61,7 @@
     groups = reach // LANES
     me, mine = lax.axis_index("row"), lax.axis_index("col")
     share = points // cols
-    kept = plan(groups, cols)
-    entries = len(kept[0])
+    kept, entries = KEPT, len(KEPT[0])
 
     barrier = pltpu.get_barrier_semaphore()
     for k in range(1, rows):
@@ -87,8 +74,14 @@
     def fetch(b, slot):
         return pltpu.make_async_copy(basis.at[b], held.at[slot], in_sem.at[slot])
 
-    for b in range(DEPTH - 1):
+    for b in range(STEP):
         fetch(b, b).start()
+
+    def chosen(values):
+        total = values[0]
+        for c in range(1, cols):
+            total = jnp.where(mine == c, values[c], total)
+        return total
 
     def rows_for(owner):
         return coeffs.at[pl.ds(pl.multiple_of(lax.rem(owner * WIN, owned), 32), WIN), :]
@@ -113,27 +106,38 @@
     load.start()
 
     start = lax.rem(me * WIN, owned)
-    row_of = lax.broadcasted_iota(jnp.int32, (WIN, 1), 0) + start
-    name = jnp.concatenate([row_of + partner(k) * owned for k in ORDER], axis=0)
+    for r in range(len(USED[0])):
+        row = lax.broadcasted_iota(jnp.int32, (LANES, LANES), 0) + chosen([g[r] for g in USED]) * LANES
+        found = jnp.zeros_like(row)
+        for p, k in enumerate(ORDER):
+            own_row = row - p * WIN
+            found = jnp.where((own_row >= 0) & (own_row < WIN), own_row + (start + partner(k) * owned), found)
+        names[r * LANES:(r + 1) * LANES, :] = found
     lane = lax.broadcasted_iota(jnp.int32, (1, slots), 1)
     atoms = lax.broadcasted_iota(jnp.int32, (1, LANES), 1)
     matrix[...] = jnp.zeros_like(matrix)
 
-    def scatter(b, carry):
-        slot = lax.rem(b, DEPTH)
-        ahead = b + DEPTH - 1
-
-        @pl.when(ahead < batches)
+    def scatter(step, carry):
+        first = step * STEP
+        base = lax.rem(step, 2) * STEP
+
+        @pl.when(first + STEP < batches)
         def _():
-            fetch(ahead, lax.rem(ahead, DEPTH)).start()
-
-        fetch(b, slot).wait()
-        ids = jnp.where(lane < count[b], index[pl.ds(b, 1), :], -1)
-        hot = jnp.where(name == ids, 1.0, 0.0).astype(jnp.bfloat16)
-        moved = lax.dot_general(hot, held[slot], (((1,), (1,)), ((), ())),
-                                preferred_element_type=jnp.float32)
-        spread[b] = moved.astype(jnp.bfloat16)
-        member[pl.ds(b, 1), :] = jnp.where(atoms == atom[b], 1.0, 0.0)
+            for u in range(STEP):
+                fetch(first + STEP + u, STEP - base + u).start()
+
+        for u in range(STEP):
+            fetch(first + u, base + u).wait()
+        for u in range(STEP):
+            b = first + u
+            ids = jnp.where(lane < count[b], index[pl.ds(b, 1), :], -1)
+            hot = jnp.concatenate(
+                [jnp.where(names[...] == ids[:, n:n + LANES], 1.0, 0.0) for n in range(0, slots, LANES)],
+                axis=1).astype(jnp.bfloat16)
+            moved = lax.dot_general(hot, held[base + u], (((1,), (1,)), ((), ())),
+                                    preferred_element_type=jnp.float32)
+            spread[b] = moved.astype(jnp.bfloat16)
+            member[pl.ds(b, 1), :] = jnp.where(lax.rem(atoms, NATOM) == atom[b], 1.0, 0.0)
         return carry
 
     def group_rows(g):
@@ -179,22 +183,31 @@
         norm[stage] = tile
         for k in range(1, cols):
             norm_copy(stage, k).start()
-        for block, (owner, slot) in spots.items():
-            i, j = block
-            if max(block) not in fresh:
-                continue
-            both = lax.dot_general(split[j], window[group_rows(i), :], (((1,), (1,)), ((), ())),
-                                   preferred_element_type=jnp.float32)
-            value = both[0:LANES, :] + both[LANES:2 * LANES, :]
-            local[ids_of[block]] = value
+        made = {}
+        for j in fresh:
+            for first in range(0, j + 1, 2):
+                lanes = range(first, min(first + 2, j + 1))
+                right = window[first * LANES:(lanes[-1] + 1) * LANES, :]
+                both = lax.dot_general(split[j], right, (((1,), (1,)), ((), ())),
+                                       preferred_element_type=jnp.float32)
+                value = both[0:LANES, :] + both[LANES:2 * LANES, :]
+                for n, i in enumerate(lanes):
+                    made[i, j] = value[:, group_rows(n)]
+        ready = [block for block in spots if max(block) in fresh]
+        for i, j in ready:
+            value = made[i, j] if i <= j else made[j, i].T
+            n = ids_of[i, j]
+            local[n] = value
             ratio = value * scale_col[j] * scale_row[i, 0:1, :]
             steps = jnp.round(ratio * STEPS).astype(jnp.int32)
             half = LANES // 2
-            code[ids_of[block]] = (steps[0:half, :] << 16) | (steps[half:, :] & 0xFFFF)
-
+            code[n] = (steps[0:half, :] << 16) | (steps[half:, :] & 0xFFFF)
+        for owner in range(cols):
             @pl.when(mine != owner)
             def _():
-                block_copy(block).start()
+                for block in ready:
+                    if spots[block][0] == owner:
+                        block_copy(block).start()
 
     def collect(owner, es):
         others = [s for s in range(cols) if s != owner]
@@ -235,7 +248,7 @@
                         send_sem=vsend_sem.at[stage, 0], recv_sem=vrecv_sem.at[s, stage],
                         device_id={"col": s}, device_id_type=MESH).wait_recv()
 
-    bounds = [batches * n // 40 for n in (0, 16, 26, 36, 40)]
+    bounds = [batches // STEP * n // 10 for n in (0, 4, 6, 8, 10)]
     arrived = 1
     own.wait()
     for stage, fresh in enumerate(stages):
@@ -245,24 +258,18 @@
             arrived += 1
         correlate(stage, fresh)
 
-    def chosen(values):
-        total = values[0]
-        for c in range(1, cols):
-            total = jnp.where(mine == c, values[c], total)
-        return total
-
     def group_of(b, g):
         return spread[b, pl.ds(pl.multiple_of(g * LANES, LANES), LANES), :]
 
     def multiply(b, es):
         total = jnp.zeros((8, points), jnp.float32)
         for e in es:
-            i = chosen([kept[c][e][0] for c in range(cols)])
+            i = chosen([USED[c].index(kept[c][e][0]) for c in range(cols)])
             right = group_of(b, i)
             product = lax.dot_general(matrix[e], jnp.concatenate([right, right], axis=0),
                                       (((1,), (0,)), ((), ())), preferred_element_type=jnp.float32)
             for h in range(2):
-                j = chosen([kept[c][e][1][min(h, len(kept[c][e][1]) - 1)] for c in range(cols)])
+                j = chosen([USED[c].index(kept[c][e][1][min(h, len(kept[c][e][1]) - 1)]) for c in range(cols)])
                 term = product[group_rows(h), :] * group_of(b, j).astype(jnp.float32)
                 total = total + jnp.sum(term.reshape(LANES // 8, 8, points), axis=0)
         return jnp.sum(total, axis=0, keepdims=True)
@@ -302,7 +309,9 @@
         for c in range(cols):
             dens[c, here, :] = values[:, c * share:(c + 1) * share]
         part = jnp.sum(angular[:, here, :] * values[None], axis=2, keepdims=True)
-        moment[...] += jnp.sum(part * member[here, :][None], axis=1)
+        packed = moment.shape[0]
+        low, high = part[:packed], part[part.shape[0] - packed:]
+        moment[...] += jnp.sum(jnp.where(atoms[None] < NATOM, low, high) * member[here, :][None], axis=1)
         return carry
 
     lax.fori_loop(0, batches // 8, late, 0)
@@ -329,10 +338,12 @@
     for stage in range(len(stages)):
         for k in range(1, cols):
             norm_copy(stage, k).wait_send()
-    for block, (owner, slot) in spots.items():
+    for owner in range(cols):
         @pl.when(mine != owner)
         def _():
-            block_copy(block).wait_send()
+            for block in spots:
+                if spots[block][0] == owner:
+                    block_copy(block).wait_send()
     for copy in moved:
         copy.wait()
     total = near[0]
@@ -352,7 +363,14 @@
     total = far[0]
     for r in range(1, rows):
         total = total + far[r]
-    out_moments[...] = total[:, :NATOM]
+    out_moments[...] = total
+
+
+def finish(density, moments, out, out_moments):
+    out[...] = density[...]
+    packed, lm = moments.shape[0], out_moments.shape[0]
+    out_moments[lm - packed:, :] = moments[:, NATOM:]
+    out_moments[:packed, :] = moments[:, :NATOM]
 
 
 def fused(coeffs, occupation, basis_on_grid, basis_map, basis_count, batch_atom, harmonics):
@@ -361,8 +379,7 @@
     rows, cols = lax.axis_size("row"), lax.axis_size("col")
     reach = rows * WIN
     groups = reach // LANES
-    kept = plan(groups, cols)
-    entries = len(kept[0])
+    entries = len(KEPT[0])
     blocks = groups * (groups + 1) // 2
     stages = groups - 2
     vmem, dma = pltpu.VMEM, pltpu.SemaphoreType.DMA
@@ -370,15 +387,17 @@
     whole = pl.BlockSpec(memory_space=pltpu.VMEM)
     scalar = pl.BlockSpec(memory_space=pltpu.SMEM)
     lm = harmonics.shape[1]
+    packed = (lm + 1) // 2
     apart = pl.BlockSpec(memory_space=pl.ANY)
     density, moments = pl.pallas_call(
         functools.partial(kernel, rows, cols, owned),
         out_shape=(jax.ShapeDtypeStruct((batches, points // cols), single),
-                   jax.ShapeDtypeStruct((lm, NATOM), single)),
+                   jax.ShapeDtypeStruct((packed, LANES), single)),
         in_specs=[apart, whole, apart, whole, scalar, scalar, apart],
         out_specs=(whole, whole),
         scratch_shapes=[
             vmem((DEPTH, points, slots), half),
+            vmem((len(USED[0]) * LANES, LANES), word),
             vmem((reach, states), half),
             vmem((groups, 2 * LANES, states), half),
             vmem((blocks, LANES, LANES), single),
@@ -389,15 +408,15 @@
             vmem((cols, 2 * entries, LANES // 2, LANES), word),
             vmem((cols, stages, 8, LANES), single),
             vmem((entries, 2 * LANES, 2 * LANES), half),
-            vmem((batches, reach, points), half),
+            vmem((batches, len(USED[0]) * LANES, points), half),
             vmem((lm, batches, points), single),
             vmem((batches, LANES), single),
             vmem((batches, points), single),
             vmem((cols, batches, points // cols), single),
             vmem((cols - 1, batches, points // cols), single),
-            vmem((cols, lm, LANES), single),
-            vmem((rows, lm, LANES), single),
-            vmem((lm, LANES), single),
+            vmem((cols, packed, LANES), single),
+            vmem((rows, packed, LANES), single),
+            vmem((packed, LANES), single),
             dma, dma((DEPTH,)), dma, dma((rows - 1,)), dma((rows - 1,)),
             dma((blocks,)), dma((cols, 2 * entries)), dma((stages, cols - 1)), dma((cols, stages)),
             dma((cols - 1,)), dma((cols - 1,)), dma((cols - 1,)), dma((cols - 1,)),
@@ -407,6 +426,10 @@
             collective_id=0, has_side_effects=True, vmem_limit_bytes=VMEM_BYTES),
     )(coeffs, occupation.reshape(1, -1), basis_on_grid, basis_map, basis_count,
       batch_atom, jnp.transpose(harmonics, (1, 0, 2)))
+    density, moments = pl.pallas_call(
+        finish, out_shape=(jax.ShapeDtypeStruct(density.shape, single),
+                           jax.ShapeDtypeStruct((lm, NATOM), single)),
+        in_specs=[whole, whole], out_specs=(whole, whole))(density, moments)
     return density, moments.T
 
 
@@ -418,7 +441,7 @@
     share = points // cols
     needed = batches * reach * points * 2 + 10 * reach * states
     fits = needed < VMEM_BYTES * 3 // 4 and share % LANES == 0 and owned % WIN == 0
-    if fits and rows == len(ORDER) and cols == 4 and reach % LANES == 0 and batches % 8 == 0:
+    if fits and rows == len(ORDER) and cols == len(KEPT) and reach == 6 * LANES and 2 * NATOM == LANES and batches % (2 * STEP) == 0:
         return fused(coeffs, occupation, basis_on_grid, basis_map, basis_count,
                      batch_atom, harmonics)
     density = plain(coeffs, occupation, basis_on_grid, basis_map, basis_count)

time: 69.1 us -> 55 us (0.80)
  Pallas kernels: 65.5 us -> 54 us
  local copies, waits for them, and re-layouts: 2.69 us -> 0 us
    pallas_call x1, Pallas kernels: 65.5 us -> 52.6 us  [fused(): pl.pallas_call(functools.partial(kernel, rows, cols, owned), out_shape=(j...]
    unnamed x2 -> x0, local copies, waits for them, and re-layouts: 2.69 us -> none
    pallas_call x0 -> x1, Pallas kernels: none -> 1.42 us  [fused(): pl.pallas_call(finish, out_shape=(jax.ShapeDtypeStruct(density.shape, sin...]
where the time goes in v2:
time: 55 us; the launch traced here: 54.6 us
  Pallas kernels  54 us (98%)
  between operations  0.64 us (1%)
    pallas_call x1, Pallas kernels, fused(): pl.pallas_call(functools.partial(kernel, rows, cols, owned), out_shape=(j...  52.6 us
    pallas_call x1, Pallas kernels, fused(): pl.pallas_call(finish, out_shape=(jax.ShapeDtypeStruct(density.shape, sin...  1.42 us

profile of v2, /device:TPU:0, one launch (start us, length us, event | category | flops | bytes accessed | tf_op | source)
XLA Modules:
  0.0 54.6 jit_solution(3001678689257558416)
XLA Ops:
  0.6 52.6 %shard_map.86 = (f32[40,128]{1,0:T(8,128)}, f32[25,128]{1,0:T(8,128)}) custom-call(bf16[768,1024]{1,0:T(8,128)(2,1)} %coeffs.1, f32[1,1024]{1,0:T(1,128)} %bitcast.4, bf16[40,512,512]{2,1,0:T(8,128)(2,1)} %basis.1, s32[40,512]{1,0:T(8,128)} %index.1, s32[40]{0:T(128)} %count.1, s32[40]{0:T(128)} %atom.1, f32[49,40,512]{2,1,0:T(8,128)} %bitcast.3), custom_call_target="tpu_custom_call" | custom-call | tf_op jit(solution)/shard_map/pallas_call | solution.py:392
  53.2 1.4 %shard_map.87 = (f32[40,128]{1,0:T(8,128)}, f32[49,64]{1,0:T(8,128)}) custom-call(f32[40,128]{1,0:T(8,128)} %get-tuple-element.6.density, f32[25,128]{1,0:T(8,128)} %get-tuple-element.7.moments), custom_call_target="tpu_custom_call" | custom-call | tf_op jit(solution)/shard_map/pallas_call | solution.py:429

commit v3 on v2

--- a/solution.py
+++ b/solution.py
@@ -19,8 +19,8 @@
 ORDER = (0, 1, 2, 4, 3, 5, 6, 7)
 KEPT = (
     ((0, (2, 3)), (1, (2, 3)), (1, (1,))),
-    ((4, (0, 1)), (0, (0, 1)), (5, (0, 1))),
-    ((4, (2, 3)), (2, (2, 3)), (5, (2, 3))),
+    ((0, (0, 1)), (4, (0, 1)), (5, (0, 1))),
+    ((2, (2, 3)), (4, (2, 3)), (5, (2, 3))),
     ((3, (3,)), (4, (4,)), (5, (4, 5))),
 )
 USED = ((0, 1, 2, 3), (0, 1, 4, 5), (2, 3, 4, 5), (2, 3, 4, 5))
@@ -50,10 +50,10 @@
     return lax.dynamic_slice_in_dim(full_density, lax.axis_index("col") * share, share, 1)
 
 
-def kernel(rows, cols, owned, coeffs, occ, basis, index, count, atom, harmonics, out, out_moments,
-           held, names, window, split, local, scale_col, scale_row, norm, code, taken, norms, matrix,
+def kernel(rows, cols, owned, coeffs, occ_in, basis, index_in, count_in, atom_in, harmonics, out, out_moments,
+           occ, index, count, atom, held, names, window, split, local, scale_col, scale_row, norm, code, taken, norms, matrix,
            spread, angular, member, line, dens, got, near, far, moment,
-           own_sem, in_sem, angular_sem, send_sem, recv_sem, zsend_sem, zrecv_sem, vsend_sem, vrecv_sem,
+           small_sem, own_sem, in_sem, angular_sem, send_sem, recv_sem, zsend_sem, zrecv_sem, vsend_sem, vrecv_sem,
            dsend_sem, drecv_sem, nsend_sem, nrecv_sem, fsend_sem, frecv_sem):
     batches, points, slots = basis.shape
     states = coeffs.shape[1]
@@ -74,6 +74,10 @@
     def fetch(b, slot):
         return pltpu.make_async_copy(basis.at[b], held.at[slot], in_sem.at[slot])
 
+    small = [pltpu.make_async_copy(src, dst, small_sem.at[n]) for n, (src, dst) in enumerate(
+        ((count_in, count), (index_in, index), (atom_in, atom), (occ_in, occ)))]
+    for copy in small:
+        copy.start()
     for b in range(STEP):
         fetch(b, b).start()
 
@@ -248,16 +252,6 @@
                         send_sem=vsend_sem.at[stage, 0], recv_sem=vrecv_sem.at[s, stage],
                         device_id={"col": s}, device_id_type=MESH).wait_recv()
 
-    bounds = [batches // STEP * n // 10 for n in (0, 4, 6, 8, 10)]
-    arrived = 1
-    own.wait()
-    for stage, fresh in enumerate(stages):
-        lax.fori_loop(bounds[stage], bounds[stage + 1], scatter, 0)
-        while arrived < needs[fresh[-1]]:
-            sends[arrived - 1].wait_recv()
-            arrived += 1
-        correlate(stage, fresh)
-
     def group_of(b, g):
         return spread[b, pl.ds(pl.multiple_of(g * LANES, LANES), LANES), :]
 
@@ -274,28 +268,41 @@
                 total = total + jnp.sum(term.reshape(LANES // 8, 8, points), axis=0)
         return jnp.sum(total, axis=0, keepdims=True)
 
+    def take(e, which):
+        for owner in range(cols):
+            @pl.when(mine == owner)
+            def _():
+                await_norms(owner, which)
+                collect(owner, [e])
+
+    def add(e):
+        def body(step, carry):
+            for u in range(8):
+                b = step * 8 + u
+                value = multiply(b, [e])
+                line[pl.ds(b, 1), :] = value if e == 0 else line[pl.ds(b, 1), :] + value
+            return carry
+
+        lax.fori_loop(0, batches // 8, body, 0)
+
     last = len(stages) - 1
-    for owner in range(cols):
-        @pl.when(mine == owner)
-        def _():
-            await_norms(owner, range(last))
-            collect(owner, range(entries - 1))
-
-    unroll = 4
-
-    def early(step, carry):
-        for u in range(unroll):
-            b = step * unroll + u
-            line[pl.ds(b, 1), :] = multiply(b, range(entries - 1))
-        return carry
-
-    lax.fori_loop(0, batches // unroll, early, 0)
-
-    for owner in range(cols):
-        @pl.when(mine == owner)
-        def _():
-            await_norms(owner, [last])
-            collect(owner, [entries - 1])
+    bounds = [batches // STEP * n // 10 for n in (0, 4, 7, 10, 10)]
+    arrived = 1
+    own.wait()
+    for copy in small:
+        copy.wait()
+    for stage, fresh in enumerate(stages):
+        lax.fori_loop(bounds[stage], bounds[stage + 1], scatter, 0)
+        if stage == last:
+            take(0, range(last - 1))
+            add(0)
+        while arrived < needs[fresh[-1]]:
+            sends[arrived - 1].wait_recv()
+            arrived += 1
+        correlate(stage, fresh)
+    take(1, [last - 1])
+    add(1)
+    take(2, [last])
 
     load.wait()
     moment[...] = jnp.zeros_like(moment)
@@ -330,8 +337,6 @@
 
     moved = exchange("col", mine, cols, lambda peer: moment, lambda k: near.at[mine],
                      nsend_sem, nrecv_sem)
-    copies = exchange("col", mine, cols, lambda peer: dens.at[peer], lambda k: got.at[k - 1],
-                      dsend_sem, drecv_sem)
     near[mine] = moment[...]
     for copy in sends:
         copy.wait_send()
@@ -353,6 +358,8 @@
     far[me] = total
     moved = exchange("row", me, rows, lambda peer: moment, lambda k: far.at[me],
                      fsend_sem, frecv_sem)
+    copies = exchange("col", mine, cols, lambda peer: dens.at[peer], lambda k: got.at[k - 1],
+                      dsend_sem, drecv_sem)
     result = dens[mine]
     for k, copy in enumerate(copies):
         copy.wait()
@@ -385,7 +392,6 @@
     vmem, dma = pltpu.VMEM, pltpu.SemaphoreType.DMA
     half, single, word = jnp.bfloat16, jnp.float32, jnp.int32
     whole = pl.BlockSpec(memory_space=pltpu.VMEM)
-    scalar = pl.BlockSpec(memory_space=pltpu.SMEM)
     lm = harmonics.shape[1]
     packed = (lm + 1) // 2
     apart = pl.BlockSpec(memory_space=pl.ANY)
@@ -393,9 +399,13 @@
         functools.partial(kernel, rows, cols, owned),
         out_shape=(jax.ShapeDtypeStruct((batches, points // cols), single),
                    jax.ShapeDtypeStruct((packed, LANES), single)),
-        in_specs=[apart, whole, apart, whole, scalar, scalar, apart],
+        in_specs=[apart] * 7,
         out_specs=(whole, whole),
         scratch_shapes=[
+            vmem((1, states), single),
+            vmem((batches, slots), word),
+            pltpu.SMEM((batches,), word),
+            pltpu.SMEM((batches,), word),
             vmem((DEPTH, points, slots), half),
             vmem((len(USED[0]) * LANES, LANES), word),
             vmem((reach, states), half),
@@ -417,7 +427,7 @@
             vmem((cols, packed, LANES), single),
             vmem((rows, packed, LANES), single),
             vmem((packed, LANES), single),
-            dma, dma((DEPTH,)), dma, dma((rows - 1,)), dma((rows - 1,)),
+            dma((4,)), dma, dma((DEPTH,)), dma, dma((rows - 1,)), dma((rows - 1,)),
             dma((blocks,)), dma((cols, 2 * entries)), dma((stages, cols - 1)), dma((cols, stages)),
             dma((cols - 1,)), dma((cols - 1,)), dma((cols - 1,)), dma((cols - 1,)),
             dma((rows - 1,)), dma((rows - 1,)),

time: 55 us -> 52.7 us (0.958)
  Pallas kernels: 54 us -> 51.8 us
    pallas_call x1, Pallas kernels: 52.6 us -> 50.3 us  [fused(): pl.pallas_call(functools.partial(kernel, rows, cols, owned), out_shape=(j...]
where the time goes in v3:
time: 52.7 us; the launch traced here: 52.4 us
  Pallas kernels  51.8 us (98%)
  between operations  0.64 us (1%)
    pallas_call x1, Pallas kernels, fused(): pl.pallas_call(functools.partial(kernel, rows, cols, owned), out_shape=(j...  50.3 us
    pallas_call x1, Pallas kernels, fused(): pl.pallas_call(finish, out_shape=(jax.ShapeDtypeStruct(density.shape, sin...  1.42 us

profile of v3, /device:TPU:0, one launch (start us, length us, event | category | flops | bytes accessed | tf_op | source)
XLA Modules:
  0.0 52.4 jit_solution(14345422491953790830)
XLA Ops:
  0.6 50.3 %shard_map.86 = (f32[40,128]{1,0:T(8,128)}, f32[25,128]{1,0:T(8,128)}) custom-call(bf16[768,1024]{1,0:T(8,128)(2,1)} %coeffs.1, f32[1,1024]{1,0:T(1,128)} %bitcast.4, bf16[40,512,512]{2,1,0:T(8,128)(2,1)} %basis.1, s32[40,512]{1,0:T(8,128)} %index_in.1, s32[40]{0:T(128)} %count_in.1, s32[40]{0:T(128)} %atom_in.1, f32[49,40,512]{2,1,0:T(8,128)} %bitcast.3), custom_call_target="tpu_custom_call" | custom-call | tf_op jit(solution)/shard_map/pallas_call | solution.py:398
  51.0 1.4 %shard_map.87 = (f32[40,128]{1,0:T(8,128)}, f32[49,64]{1,0:T(8,128)}) custom-call(f32[40,128]{1,0:T(8,128)} %get-tuple-element.6.density, f32[25,128]{1,0:T(8,128)} %get-tuple-element.7.moments), custom_call_target="tpu_custom_call" | custom-call | tf_op jit(solution)/shard_map/pallas_call | solution.py:439

commit v4 on v3

--- a/solution.py
+++ b/solution.py
@@ -286,7 +286,7 @@
         lax.fori_loop(0, batches // 8, body, 0)
 
     last = len(stages) - 1
-    bounds = [batches // STEP * n // 10 for n in (0, 4, 7, 10, 10)]
+    bounds = [batches // STEP * n // 10 for n in (0, 3, 6, 10, 10)]
     arrived = 1
     own.wait()
     for copy in small:

time: 52.7 us -> 53.3 us (1.011)
    pallas_call x1, Pallas kernels: 50.3 us -> 50.9 us  [fused(): pl.pallas_call(functools.partial(kernel, rows, cols, owned), out_shape=(j...]
where the time goes in v4:
time: 53.3 us; the launch traced here: 53 us
  Pallas kernels  52.3 us (98%)
  between operations  0.64 us (1%)
    pallas_call x1, Pallas kernels, fused(): pl.pallas_call(functools.partial(kernel, rows, cols, owned), out_shape=(j...  50.9 us
    pallas_call x1, Pallas kernels, fused(): pl.pallas_call(finish, out_shape=(jax.ShapeDtypeStruct(density.shape, sin...  1.42 us

profile of v4, /device:TPU:0, one launch (start us, length us, event | category | flops | bytes accessed | tf_op | source)
XLA Modules:
  0.0 53.0 jit_solution(15186311133724987274)
XLA Ops:
  0.6 50.9 %shard_map.86 = (f32[40,128]{1,0:T(8,128)}, f32[25,128]{1,0:T(8,128)}) custom-call(bf16[768,1024]{1,0:T(8,128)(2,1)} %coeffs.1, f32[1,1024]{1,0:T(1,128)} %bitcast.4, bf16[40,512,512]{2,1,0:T(8,128)(2,1)} %basis.1, s32[40,512]{1,0:T(8,128)} %index_in.1, s32[40]{0:T(128)} %count_in.1, s32[40]{0:T(128)} %atom_in.1, f32[49,40,512]{2,1,0:T(8,128)} %bitcast.3), custom_call_target="tpu_custom_call" | custom-call | tf_op jit(solution)/shard_map/pallas_call | solution.py:398
  51.5 1.4 %shard_map.87 = (f32[40,128]{1,0:T(8,128)}, f32[49,64]{1,0:T(8,128)}) custom-call(f32[40,128]{1,0:T(8,128)} %get-tuple-element.6.density, f32[25,128]{1,0:T(8,128)} %get-tuple-element.7.moments), custom_call_target="tpu_custom_call" | custom-call | tf_op jit(solution)/shard_map/pallas_call | solution.py:439
